TPU v7x, 32 devices: a whole 2x2x4 slice. The times are simulated.
32 devices in a mesh: hyp: 2 (over x), rows: 16 (over z, y, core).
Axes of the slice: x: 2, y: 2, z: 4, core: 2. Of those that a mesh axis runs over, the one named last changes fastest.
Arguments:
- offsets: float32 [2, 65536], P(None, 'rows'), may hold values from 0 to 1
- tile_cell: int32 [512], P('rows'), may hold values from 0 to 31, as said below
- probes: int32 [8, 65536], P(None, 'rows'), may hold values from 0 to 1
- target: float32 [65536], P('rows'), may hold values from -6 to 6
- lengthscale: float32 [2], P('hyp'), parts along dimension 0, may hold values from 0.5 to 1
- amplitude: float32 [2], P('hyp'), parts along dimension 0, may hold values from 0.02 to 0.08
- noise: float32 [2], P('hyp'), parts along dimension 0, may hold values from 0.1 to 0.4
Outputs:
- solutions: float32 [18, 65536], P('hyp', 'rows'), parts along dimension 0
- quadratic: float32 [18], P('hyp'), parts along dimension 0
There are 2 independent parts, one for each index of `hyp`. A program takes and returns all parts, laid end to end along the dimension named above; an argument that names none is the same for every part. Nothing has to cross between parts.
Inputs may be any that keep to these rules, and one draw needn't show every extreme that they name: `tile_cell`: each aligned block of 32 entries (one device's tiles) is a permutation of 0 to 31.
All inputs are finite; a program needn't handle non-finite values.
Results may differ from a plain program's by a relative error of at most 0.0003.
Values sent between devices are 32-bit elements; how exact they have to be, the bound alone decides.
A program may use at most 64 MiB of HBM per device.

v0:
```python
import jax
import jax.numpy as jnp
from jax import lax
from jax.sharding import PartitionSpec as P

TILE = 128
GX = 16
ITERS = 3


def with_halo(cells, sides, width):
    for axis, dim in sides:
        count = lax.axis_size(axis)
        ends = count - 1
        head = lax.slice_in_dim(cells, 0, width, axis=dim)
        tail = lax.slice_in_dim(cells, cells.shape[dim] - width, cells.shape[dim], axis=dim)
        cells = jnp.concatenate(
            [
                lax.ppermute(tail, axis, [(i, (i + 1) % count) for i in range(ends)]),
                cells,
                lax.ppermute(head, axis, [((i + 1) % count, i) for i in range(ends)]),
            ],
            axis=dim,
        )
    return cells


def wendland(distance):
    closeness = jnp.maximum(1.0 - distance, 0.0)
    return closeness**4 * (4.0 * distance + 1.0)


def shifted_terms(
    padded_vectors,
    padded_coords,
    coords,
    row_start,
    row_count,
    row_shifts,
    inverse_length,
    amplitude,
):
    col_count = coords.shape[2]
    total = jnp.zeros(
        (padded_vectors.shape[0], row_count, col_count, padded_vectors.shape[3]), jnp.float32
    )
    for row_shift in row_shifts:
        low = 1 + row_start + row_shift
        for col_shift in (-1, 0, 1):
            other = padded_coords[
                :, low : low + row_count, 1 + col_shift : 1 + col_shift + col_count, :
            ]
            values = padded_vectors[
                :, low : low + row_count, 1 + col_shift : 1 + col_shift + col_count, :
            ]
            delta_rows = coords[0][..., :, None] - other[0][..., None, :]
            delta_cols = coords[1][..., :, None] - other[1][..., None, :]
            distance = jnp.sqrt(delta_rows * delta_rows + delta_cols * delta_cols) * inverse_length
            weights = amplitude * wendland(distance)
            total = total + jnp.einsum(
                "rabj,abij->rabi", values, weights, precision=lax.Precision.HIGHEST
            )
    return total


def widen(scalars):
    return scalars[:, None, None, None]


def local_sum(first, second):
    return jnp.sum(first * second, axis=(1, 2, 3))


def rim_vectors(vectors):
    extended = with_halo(vectors, (("rows", 1),), 1)
    return jnp.pad(extended, ((0, 0), (0, 0), (1, 1), (0, 0)))


def shards(offsets, tile_cell, probes, target, lengthscale, amplitude, noise):
    tile_count = tile_cell.shape[0]
    strip_rows = tile_count // GX
    order = jnp.argsort(tile_cell)

    def to_grid(stored):
        lead = stored.shape[0]
        return stored.reshape(lead, tile_count, TILE)[:, order].reshape(lead, strip_rows, GX, TILE)

    grid_offsets = to_grid(offsets)
    rim_offsets = with_halo(grid_offsets, (("rows", 1),), 1)
    rim_offsets = jnp.pad(rim_offsets, ((0, 0), (0, 0), (1, 1), (0, 0)))
    row_place = (jnp.arange(strip_rows + 2, dtype=jnp.int32) - 1).astype(jnp.float32)[:, None, None]
    col_place = (jnp.arange(GX + 2, dtype=jnp.int32) - 1).astype(jnp.float32)[None, :, None]
    padded_coords = jnp.stack([rim_offsets[0] + row_place, rim_offsets[1] + col_place])
    coords = padded_coords[:, 1:-1, 1:-1, :]
    inverse_length = 1.0 / lengthscale[0]
    scale_amp = amplitude[0]
    scale_noise = noise[0]

    def operate(vectors):
        extended = rim_vectors(vectors)
        total = shifted_terms(
            extended, padded_coords, coords, 0, strip_rows, (-1, 0, 1), inverse_length, scale_amp
        )
        return scale_noise * vectors + total

    signs = 2.0 * probes.astype(jnp.float32) - 1.0
    right_sides = to_grid(jnp.concatenate([signs, target[None, :]], axis=0))
    iterate = jnp.zeros_like(right_sides)
    residual = right_sides

    def paired_sums(current):
        image_now = operate(current)
        totals = lax.psum((local_sum(current, current), local_sum(current, image_now)), "rows")
        return (image_now, totals[0], totals[1])

    image, norm_now, product = paired_sums(residual)
    alpha = norm_now / product
    direction = residual
    along = image
    for iteration in range(ITERS):
        iterate = iterate + widen(alpha) * direction
        residual = residual - widen(alpha) * along
        if iteration + 1 < ITERS:
            image, norm_next, product = paired_sums(residual)
            ratio = norm_next / norm_now
            alpha = norm_next / (product - ratio * norm_next / alpha)
            direction = residual + widen(ratio) * direction
            along = image + widen(ratio) * along
            norm_now = norm_next
    point_total = tile_count * TILE * lax.axis_size("rows")
    quadratic = lax.psum(local_sum(right_sides, iterate), "rows") / point_total
    solutions = iterate.reshape(iterate.shape[0], tile_count, TILE)[:, tile_cell].reshape(
        iterate.shape[0], tile_count * TILE
    )
    return (solutions, quadratic)


def solution(mesh):
    return jax.shard_map(
        shards,
        mesh=mesh,
        in_specs=(
            P(None, "rows"),
            P("rows"),
            P(None, "rows"),
            P("rows"),
            P("hyp"),
            P("hyp"),
            P("hyp"),
        ),
        out_specs=(P("hyp", "rows"), P("hyp")),
        check_vma=False,
    )
```

profile of v0, /device:TPU:0, one launch (start us, length us, event | category | flops | bytes accessed | tf_op | source)
XLA Modules:
  0.0 302.0 jit_solution(14213078919314780951)
XLA Ops:
  24.6 5.4 %convolution_add_fusion.20 = f32[2,16,128,9]{2,3,1,0:T(8,128)S(1)} fusion(f32[2,16,128,9]{2,3,1,0:T(8,128)S(1)} %fusion.13, f32[]{:T(128)} %bitcast.15, f32[2,16,128]{2,1,0:T(8,128)S(1)} %bitcast.193, f32[2,16,128]{2,1,0:T(8,128)S(1)} %bitcast.137, f32[2,16,128]{2,1,0:T(8,128)S(1)} %bitcast.190, f32[2,16,128]{2,1,0:T(8,128)S(1)} %bitcast.110, f32[]{:T(128)} %bitcast.62, ...), kind=kOutput, calls=%fused_computation.38 | convolution fusion | flops 64000000 | bytes 737288 | tf_op jit(solution)/shard_map/rabj,abij->rabi/dot_general | solution.py:60
  30.0 5.4 %convolution_add_fusion.19 = f32[2,16,128,9]{2,3,1,0:T(8,128)S(1)} fusion(f32[2,16,128,9]{2,3,1,0:T(8,128)S(1)} %convolution_add_fusion.20, f32[2,16,128]{2,1,0:T(8,128)S(1)} %bitcast.187, f32[2,16,128]{2,1,0:T(8,128)S(1)} %bitcast.184, f32[]{:T(128)} %bitcast.15, f32[2,16,128]{2,1,0:T(8,128)S(1)} %bitcast.138, f32[2,16,128]{2,1,0:T(8,128)S(1)} %bitcast.111, ...), kind=kOutput, calls=%fused_computation.37 | convolution fusion | flops 64000000 | bytes 737288 | tf_op jit(solution)/shard_map/rabj,abij->rabi/dot_general | solution.py:60
  35.4 5.4 %convolution_add_fusion.18 = f32[2,16,128,9]{2,3,1,0:T(8,128)S(1)} fusion(f32[2,16,128,9]{2,3,1,0:T(8,128)S(1)} %convolution_add_fusion.19, f32[2,16,128]{2,1,0:T(8,128)S(1)} %bitcast.181, f32[2,16,128]{2,1,0:T(8,128)S(1)} %bitcast.178, f32[]{:T(128)} %bitcast.15, f32[2,16,128]{2,1,0:T(8,128)S(1)} %bitcast.139, f32[2,16,128]{2,1,0:T(8,128)S(1)} %bitcast.112, ...), kind=kOutput, calls=%fused_computation.36 | convolution fusion | flops 64000000 | bytes 737288 | tf_op jit(solution)/shard_map/rabj,abij->rabi/dot_general | solution.py:60
  51.1 5.4 %convolution_add_fusion.16 = f32[2,16,128,9]{2,3,1,0:T(8,128)S(1)} fusion(f32[2,16,128,9]{2,3,1,0:T(8,128)S(1)} %convolution_add_fusion.17, f32[2,16,128]{2,1,0:T(8,128)S(1)} %bitcast.175, f32[2,16,128]{2,1,0:T(8,128)S(1)} %bitcast.172, f32[]{:T(128)} %bitcast.15, f32[2,16,128]{2,1,0:T(8,128)S(1)} %bitcast.142, f32[2,16,128]{2,1,0:T(8,128)S(1)} %bitcast.115, ...), kind=kOutput, calls=%fused_computation.34 | convolution fusion | flops 64000000 | bytes 737288 | tf_op jit(solution)/shard_map/rabj,abij->rabi/dot_general | solution.py:60
  56.5 5.4 %convolution_add_fusion.15 = f32[2,16,128,9]{2,3,1,0:T(8,128)S(1)} fusion(f32[2,16,128,9]{2,3,1,0:T(8,128)S(1)} %convolution_add_fusion.16, f32[2,16,128]{2,1,0:T(8,128)S(1)} %bitcast.169, f32[2,16,128]{2,1,0:T(8,128)S(1)} %bitcast.166, f32[]{:T(128)} %bitcast.15, f32[2,16,128]{2,1,0:T(8,128)S(1)} %bitcast.143, f32[2,16,128]{2,1,0:T(8,128)S(1)} %bitcast.116, ...), kind=kOutput, calls=%fused_computation.33 | convolution fusion | flops 64000000 | bytes 737288 | tf_op jit(solution)/shard_map/rabj,abij->rabi/dot_general | solution.py:60
  61.8 5.6 %multiply_reduce_fusion.4 = (f32[9]{0:T(128)S(1)}, f32[9,2,16,128]{3,0,2,1:T(8,128)S(1)}) fusion(f32[9,2,16,128]{3,0,2,1:T(8,128)S(1)} %bitcast.97, f32[2,16,128,9]{2,3,1,0:T(8,128)S(1)} %fusion.16, f32[2,16,128,9]{2,3,1,0:T(8,128)S(1)} %convolution_add_fusion.15, f32[9,1,16,128]{3,0,2,1:T(8,128)S(1)} %collective-permute-done.3, ...), kind=kOutput, calls=%fused_computation.99 | convolution fusion | flops 64221176 | bytes 729136 | tf_op jit(solution)/shard_map/rabj,abij->rabi/dot_general | solution.py:60
  67.4 34.2 %all-reduce.6 = (f32[9]{0:T(128)S(1)}, f32[9]{0:T(128)S(1)}) all-reduce(f32[9]{0:T(128)S(1)} %fusion.42, f32[9]{0:T(128)S(1)} %get-tuple-element.47), channel_id=1, replica_groups=mesh['hyp'=2,'rows'=16] {'rows'}, use_global_device_ids=true, to_apply=%region_2.3 | all-reduce | flops 18 | bytes 144 | tf_op jit(solution)/shard_map/psum | solution.py:113
  111.7 5.4 %fusion.12 = f32[2,16,128,9]{2,3,1,0:T(8,128)S(1)} fusion(f32[2,16,128]{2,1,0:T(8,128)S(1)} %bitcast.200, f32[2,16,128]{2,1,0:T(8,128)S(1)} %bitcast.197, f32[]{:T(128)} %bitcast.15, f32[2,16,128]{2,1,0:T(8,128)S(1)} %bitcast.146, f32[2,16,128]{2,1,0:T(8,128)S(1)} %bitcast.119, f32[]{:T(128)} %bitcast.76, ...), kind=kOutput, calls=%fused_computation.45 | convolution fusion | flops 64000000 | bytes 434184 | tf_op jit(solution)/shard_map/rabj,abij->rabi/dot_general | solution.py:60
  117.1 5.4 %convolution_add_fusion.13 = f32[2,16,128,9]{2,3,1,0:T(8,128)S(1)} fusion(f32[2,16,128,9]{2,3,1,0:T(8,128)S(1)} %fusion.12, f32[]{:T(128)} %bitcast.15, f32[2,16,128]{2,1,0:T(8,128)S(1)} %bitcast.194, f32[2,16,128]{2,1,0:T(8,128)S(1)} %bitcast.147, f32[2,16,128]{2,1,0:T(8,128)S(1)} %bitcast.191, f32[2,16,128]{2,1,0:T(8,128)S(1)} %bitcast.120, f32[]{:T(128)} %bitcast.74, ...), kind=kOutput, calls=%fused_computation.29 | convolution fusion | flops 64000000 | bytes 737288 | tf_op jit(solution)/shard_map/rabj,abij->rabi/dot_general | solution.py:60
  122.5 5.4 %convolution_add_fusion.12 = f32[2,16,128,9]{2,3,1,0:T(8,128)S(1)} fusion(f32[2,16,128,9]{2,3,1,0:T(8,128)S(1)} %convolution_add_fusion.13, f32[2,16,128]{2,1,0:T(8,128)S(1)} %bitcast.188, f32[2,16,128]{2,1,0:T(8,128)S(1)} %bitcast.185, f32[]{:T(128)} %bitcast.15, f32[2,16,128]{2,1,0:T(8,128)S(1)} %bitcast.148, f32[2,16,128]{2,1,0:T(8,128)S(1)} %bitcast.121, ...), kind=kOutput, calls=%fused_computation.28 | convolution fusion | flops 64000000 | bytes 737288 | tf_op jit(solution)/shard_map/rabj,abij->rabi/dot_general | solution.py:60
  127.9 5.4 %convolution_add_fusion.11 = f32[2,16,128,9]{2,3,1,0:T(8,128)S(1)} fusion(f32[2,16,128,9]{2,3,1,0:T(8,128)S(1)} %convolution_add_fusion.12, f32[2,16,128]{2,1,0:T(8,128)S(1)} %bitcast.182, f32[2,16,128]{2,1,0:T(8,128)S(1)} %bitcast.179, f32[]{:T(128)} %bitcast.15, f32[2,16,128]{2,1,0:T(8,128)S(1)} %bitcast.149, f32[2,16,128]{2,1,0:T(8,128)S(1)} %bitcast.122, ...), kind=kOutput, calls=%fused_computation.27 | convolution fusion | flops 64000000 | bytes 737288 | tf_op jit(solution)/shard_map/rabj,abij->rabi/dot_general | solution.py:60
  138.2 5.4 %convolution_add_fusion.9 = f32[2,16,128,9]{2,3,1,0:T(8,128)S(1)} fusion(f32[2,16,128,9]{2,3,1,0:T(8,128)S(1)} %convolution_add_fusion.10, f32[2,16,128]{2,1,0:T(8,128)S(1)} %bitcast.176, f32[2,16,128]{2,1,0:T(8,128)S(1)} %bitcast.173, f32[]{:T(128)} %bitcast.15, f32[2,16,128]{2,1,0:T(8,128)S(1)} %bitcast.151, f32[2,16,128]{2,1,0:T(8,128)S(1)} %bitcast.124, ...), kind=kOutput, calls=%fused_computation.25 | convolution fusion | flops 64000000 | bytes 737288 | tf_op jit(solution)/shard_map/rabj,abij->rabi/dot_general | solution.py:60
  143.6 5.4 %convolution_add_fusion.8 = f32[2,16,128,9]{2,3,1,0:T(8,128)S(1)} fusion(f32[2,16,128,9]{2,3,1,0:T(8,128)S(1)} %convolution_add_fusion.9, f32[2,16,128]{2,1,0:T(8,128)S(1)} %bitcast.170, f32[2,16,128]{2,1,0:T(8,128)S(1)} %bitcast.167, f32[]{:T(128)} %bitcast.15, f32[2,16,128]{2,1,0:T(8,128)S(1)} %bitcast.152, f32[2,16,128]{2,1,0:T(8,128)S(1)} %bitcast.125, ...), kind=kOutput, calls=%fused_computation.24 | convolution fusion | flops 64000000 | bytes 737288 | tf_op jit(solution)/shard_map/rabj,abij->rabi/dot_general | solution.py:60
  149.0 5.6 %multiply_reduce_fusion.2 = (f32[9]{0:T(128)S(1)}, f32[9]{0:T(128)S(1)}, f32[9,2,16,128]{3,0,2,1:T(8,128)S(1)}) fusion(f32[9,2,16,128]{3,0,2,1:T(8,128)S(1)} %multiply_subtract_fusion.1, f32[2,16,128,9]{2,3,1,0:T(8,128)S(1)} %fusion.15, f32[2,16,128,9]{2,3,1,0:T(8,128)S(1)} %convolution_add_fusion.8, f32[9,1,16,128]{3,0,2,1:T(8,128)S(1)} %collective-permute-done.5, ...), kind=kOutput, calls=%fused_computation.96 | convolution fusion | flops 64294896 | bytes 729172 | tf_op jit(solution)/shard_map/rabj,abij->rabi/dot_general | solution.py:60
  154.5 30.3 %all-reduce.5 = (f32[9]{0:T(128)S(1)}, f32[9]{0:T(128)S(1)}) all-reduce(f32[9]{0:T(128)S(1)} %get-tuple-element.5, f32[9]{0:T(128)S(1)} %get-tuple-element.4), channel_id=1, replica_groups=mesh['hyp'=2,'rows'=16] {'rows'}, use_global_device_ids=true, to_apply=%region_6.7 | all-reduce | flops 18 | bytes 144 | tf_op jit(solution)/shard_map/psum | solution.py:113
  195.1 5.4 %fusion.11 = f32[2,16,128,9]{2,3,1,0:T(8,128)S(1)} fusion(f32[2,16,128]{2,1,0:T(8,128)S(1)} %bitcast.201, f32[2,16,128]{2,1,0:T(8,128)S(1)} %bitcast.198, f32[]{:T(128)} %bitcast.15, f32[2,16,128]{2,1,0:T(8,128)S(1)} %bitcast.155, f32[2,16,128]{2,1,0:T(8,128)S(1)} %bitcast.128, f32[]{:T(128)} %bitcast.75, f32[9,2,16,128]{3,0,2,1:T(8,128)S(1)} %get-tuple-element.15, ...), kind=kOutput, calls=%fused_computation.44 | convolution fusion | flops 64000000 | bytes 434184 | tf_op jit(solution)/shard_map/rabj,abij->rabi/dot_general | solution.py:60
  200.5 5.4 %convolution_add_fusion.6 = f32[2,16,128,9]{2,3,1,0:T(8,128)S(1)} fusion(f32[2,16,128,9]{2,3,1,0:T(8,128)S(1)} %fusion.11, f32[]{:T(128)} %bitcast.15, f32[2,16,128]{2,1,0:T(8,128)S(1)} %bitcast.195, f32[2,16,128]{2,1,0:T(8,128)S(1)} %bitcast.156, f32[2,16,128]{2,1,0:T(8,128)S(1)} %bitcast.192, f32[2,16,128]{2,1,0:T(8,128)S(1)} %bitcast.129, f32[]{:T(128)} %bitcast.73, ...), kind=kOutput, calls=%fused_computation.20 | convolution fusion | flops 64000000 | bytes 737288 | tf_op jit(solution)/shard_map/rabj,abij->rabi/dot_general | solution.py:60
  205.9 5.4 %convolution_add_fusion.5 = f32[2,16,128,9]{2,3,1,0:T(8,128)S(1)} fusion(f32[2,16,128,9]{2,3,1,0:T(8,128)S(1)} %convolution_add_fusion.6, f32[2,16,128]{2,1,0:T(8,128)S(1)} %bitcast.189, f32[2,16,128]{2,1,0:T(8,128)S(1)} %bitcast.186, f32[]{:T(128)} %bitcast.15, f32[2,16,128]{2,1,0:T(8,128)S(1)} %bitcast.157, f32[2,16,128]{2,1,0:T(8,128)S(1)} %bitcast.130, ...), kind=kOutput, calls=%fused_computation.19 | convolution fusion | flops 64000000 | bytes 737288 | tf_op jit(solution)/shard_map/rabj,abij->rabi/dot_general | solution.py:60
  211.3 5.4 %convolution_add_fusion.4 = f32[2,16,128,9]{2,3,1,0:T(8,128)S(1)} fusion(f32[2,16,128,9]{2,3,1,0:T(8,128)S(1)} %convolution_add_fusion.5, f32[2,16,128]{2,1,0:T(8,128)S(1)} %bitcast.183, f32[2,16,128]{2,1,0:T(8,128)S(1)} %bitcast.180, f32[]{:T(128)} %bitcast.15, f32[2,16,128]{2,1,0:T(8,128)S(1)} %bitcast.158, f32[2,16,128]{2,1,0:T(8,128)S(1)} %bitcast.131, ...), kind=kOutput, calls=%fused_computation.18 | convolution fusion | flops 64000000 | bytes 737288 | tf_op jit(solution)/shard_map/rabj,abij->rabi/dot_general | solution.py:60
  221.6 5.4 %convolution_add_fusion.2 = f32[2,16,128,9]{2,3,1,0:T(8,128)S(1)} fusion(f32[2,16,128,9]{2,3,1,0:T(8,128)S(1)} %convolution_add_fusion.3, f32[2,16,128]{2,1,0:T(8,128)S(1)} %bitcast.177, f32[2,16,128]{2,1,0:T(8,128)S(1)} %bitcast.174, f32[]{:T(128)} %bitcast.15, f32[2,16,128]{2,1,0:T(8,128)S(1)} %bitcast.160, f32[2,16,128]{2,1,0:T(8,128)S(1)} %bitcast.133, ...), kind=kOutput, calls=%fused_computation.16 | convolution fusion | flops 64000000 | bytes 737288 | tf_op jit(solution)/shard_map/rabj,abij->rabi/dot_general | solution.py:60
  227.0 5.4 %convolution_add_fusion.1 = f32[2,16,128,9]{2,3,1,0:T(8,128)S(1)} fusion(f32[2,16,128,9]{2,3,1,0:T(8,128)S(1)} %convolution_add_fusion.2, f32[2,16,128]{2,1,0:T(8,128)S(1)} %bitcast.171, f32[2,16,128]{2,1,0:T(8,128)S(1)} %bitcast.168, f32[]{:T(128)} %bitcast.15, f32[2,16,128]{2,1,0:T(8,128)S(1)} %bitcast.161, f32[2,16,128]{2,1,0:T(8,128)S(1)} %bitcast.134, ...), kind=kOutput, calls=%fused_computation.15 | convolution fusion | flops 64000000 | bytes 737288 | tf_op jit(solution)/shard_map/rabj,abij->rabi/dot_general | solution.py:60
  232.4 5.5 %fusion.10 = f32[9]{0:T(128)S(1)} fusion(f32[9,2,16,128]{3,0,2,1:T(8,128)S(1)} %get-tuple-element.15, f32[2,16,128,9]{2,3,1,0:T(8,128)S(1)} %fusion.14, f32[2,16,128,9]{2,3,1,0:T(8,128)S(1)} %convolution_add_fusion.1, f32[2,16,128]{2,1,0:T(8,128)S(1)} %bitcast.165, f32[2,16,128]{2,1,0:T(8,128)S(1)} %bitcast.108, f32[]{:T(128)} %bitcast.15, ...), kind=kOutput, calls=%fused_computation.43 | convolution fusion | flops 64221176 | bytes 581680 | tf_op jit(solution)/shard_map/rabj,abij->rabi/dot_general | solution.py:60
  237.9 32.2 %all-reduce.4 = (f32[9]{0:T(128)S(1)}, f32[9]{0:T(128)S(1)}) all-reduce(f32[9]{0:T(128)S(1)} %get-tuple-element.14, f32[9]{0:T(128)S(1)} %fusion.10), channel_id=1, replica_groups=mesh['hyp'=2,'rows'=16] {'rows'}, use_global_device_ids=true, to_apply=%region_10.11 | all-reduce | flops 18 | bytes 144 | tf_op jit(solution)/shard_map/psum | solution.py:113
  272.0 29.5 %psum.55 = f32[9]{0:T(128)S(1)} all-reduce(f32[9]{0:T(128)S(1)} %multiply_reduce_fusion), channel_id=1, replica_groups=mesh['hyp'=2,'rows'=16] {'rows'}, use_global_device_ids=true, to_apply=%region_14.15 | all-reduce | flops 9 | bytes 72 | tf_op jit(solution)/shard_map/psum | solution.py:131
  (62 shorter events, 64.7 us)
Async XLA Ops:
  0.6 2.3 copy-start
  3.6 14.6 %collective-permute-start = (f32[2,1,16,128]{3,0,2,1:T(2,128)S(1)}, f32[2,1,16,128]{3,0,2,1:T(2,128)S(1)}, u32[]{:S(2)}, u32[]{:S(2)}) collective-permute-start(f32[2,1,16,128]{3,0,2,1:T(2,128)S(1)} %get-tuple-element.45), channel_id=1, source_target_pairs={{0,1},{1,2},{2,3},{3,4},{4,5},{5,6},{6,7},{7,8},{8,9},{9,10},{10,1... | collective-permute-start | bytes 49160 | tf_op jit(solution)/shard_map/ppermute | solution.py:19
  6.0 12.2 %collective-permute-start.1 = (f32[2,1,16,128]{3,0,2,1:T(2,128)S(1)}, f32[2,1,16,128]{3,0,2,1:T(2,128)S(1)}, u32[]{:S(2)}, u32[]{:S(2)}) collective-permute-start(f32[2,1,16,128]{3,0,2,1:T(2,128)S(1)} %get-tuple-element.46), channel_id=1, source_target_pairs={{1,0},{2,1},{3,2},{4,3},{5,4},{6,5},{7,6},{8,7},{9,8},{10,9},{11,1... | collective-permute-start | bytes 49160 | tf_op jit(solution)/shard_map/ppermute | solution.py:21
  9.5 9.0 %collective-permute-start.2 = (f32[9,1,16,128]{3,0,2,1:T(8,128)S(1)}, f32[9,1,16,128]{3,0,2,1:T(8,128)S(1)}, u32[]{:S(2)}, u32[]{:S(2)}) collective-permute-start(f32[9,1,16,128]{3,0,2,1:T(8,128)S(1)} %get-tuple-element.23), channel_id=1, source_target_pairs={{0,1},{1,2},{2,3},{3,4},{4,5},{5,6},{6,7},{7,8},{8,9},{9,10},{10,1... | collective-permute-start | bytes 221192 | tf_op jit(solution)/shard_map/ppermute | solution.py:19
  14.7 4.5 %collective-permute-start.3 = (f32[9,1,16,128]{3,0,2,1:T(8,128)S(1)}, f32[9,1,16,128]{3,0,2,1:T(8,128)S(1)}, u32[]{:S(2)}, u32[]{:S(2)}) collective-permute-start(f32[9,1,16,128]{3,0,2,1:T(8,128)S(1)} %get-tuple-element.24), channel_id=1, source_target_pairs={{1,0},{2,1},{3,2},{4,3},{5,4},{6,5},{7,6},{8,7},{9,8},{10,9},{11,1... | collective-permute-start | bytes 221192 | tf_op jit(solution)/shard_map/ppermute | solution.py:21
  101.6 2.9 copy-start.1
  101.8 2.8 collective-permute-start.4
  103.1 3.2 %collective-permute-start.5 = (f32[9,1,16,128]{3,0,2,1:T(8,128)S(1)}, f32[9,1,16,128]{3,0,2,1:T(8,128)S(1)}, u32[]{:S(2)}, u32[]{:S(2)}) collective-permute-start(f32[9,1,16,128]{3,0,2,1:T(8,128)S(1)} %get-tuple-element.22), channel_id=1, source_target_pairs={{1,0},{2,1},{3,2},{4,3},{5,4},{6,5},{7,6},{8,7},{9,8},{10,9},{11,1... | collective-permute-start | bytes 221192 | tf_op jit(solution)/shard_map/ppermute | solution.py:21
  185.2 2.8 collective-permute-start.6
  186.5 3.2 %collective-permute-start.7 = (f32[9,1,16,128]{3,0,2,1:T(8,128)S(1)}, f32[9,1,16,128]{3,0,2,1:T(8,128)S(1)}, u32[]{:S(2)}, u32[]{:S(2)}) collective-permute-start(f32[9,1,16,128]{3,0,2,1:T(8,128)S(1)} %get-tuple-element.20), channel_id=1, source_target_pairs={{1,0},{2,1},{3,2},{4,3},{5,4},{6,5},{7,6},{8,7},{9,8},{10,9},{11,1... | collective-permute-start | bytes 221192 | tf_op jit(solution)/shard_map/ppermute | solution.py:21
where the time goes:
time: 302 us
  matrix products  144 us (48%)
  blocking collectives  126 us (42%)
  starting transfers between devices  15.7 us (5%)
  other arithmetic  5.59 us (2%)
  waiting for transfers between devices  4.11 us (1%)
  between operations  3.09 us (1%)
    dot_general x27, matrix products, shifted_terms(): jnp.einsum('rabj,abij->rabi', values, weights, precision=lax.Precision.HI...  144 us
    psum x3, blocking collectives, paired_sums(): lax.psum((local_sum(current, current), local_sum(current, image_now)), 'r...  96.7 us
    psum x1, blocking collectives, shards(): quadratic = lax.psum(local_sum(right_sides, iterate), 'rows') / point_total  29.5 us
    ppermute x4, starting transfers between devices, with_halo(): lax.ppermute(tail, axis, [(i, (i + 1) % count) for i in range(ends)])  10.2 us
  transfers between devices with their start and end apart: 8, of which 3 were waited for; matrix products, arithmetic and copies ran while one was open for 1% of the time, Pallas kernels for 0%

commit v1 on v0

v1 whole, which is shorter than its diff:
```python
import functools

import jax
import jax.numpy as jnp
from jax import lax
from jax.experimental import pallas as pl
from jax.experimental.pallas import tpu as pltpu
from jax.sharding import PartitionSpec as P

TILE = 128
GX = 16
RHS = 9
PAD = 16
FAR = 1.0e3
TINY = 1.0e-30
MESH = pl.DeviceIdType.MESH
F32 = jnp.float32
BF16 = jnp.bfloat16


def kernel(
    n, rows, points,
    order, cell, length, amp_ref, noise_ref, off, probes, target,
    x_ref, q_ref,
    tiles, pk, hv, vx, whi, wlo, sc, cm, acc, mom, gathered,
    halo_send, halo_recv, mom_send, mom_recv,
):
    me = lax.axis_index("rows")
    has = (me > 0, me < n - 1)
    row_lanes = GX * TILE
    reach = 3 * TILE
    amp = amp_ref[0]
    shift = amp + noise_ref[0]

    barrier = pltpu.get_barrier_semaphore()

    def greet(k, carry):
        pl.semaphore_signal(
            barrier, inc=1, device_id={"rows": lax.rem(me + k, n)}, device_id_type=MESH
        )
        return carry

    lax.fori_loop(1, n, greet, 0)

    for g in range(rows * GX):
        lanes = slice(g * TILE, (g + 1) * TILE)
        tiles[g] = jnp.concatenate(
            [
                2.0 * probes[:, lanes].astype(F32) - 1.0,
                target[:, lanes],
                off[:, lanes],
                jnp.zeros((PAD - RHS - 2, TILE), F32),
            ],
            axis=0,
        )
    for g in range(rows * GX):
        pk[0, :, g * TILE : (g + 1) * TILE] = tiles[order[g]]

    pl.semaphore_wait(barrier, n - 1)

    def halo_copy(k, side):
        first = 0 if side == 0 else (rows - 1) * row_lanes
        return pltpu.make_async_remote_copy(
            src_ref=pk.at[k, :, pl.ds(first, row_lanes)],
            dst_ref=hv.at[k, 1 - side],
            send_sem=halo_send.at[k, side],
            recv_sem=halo_recv.at[k, 1 - side],
            device_id={"rows": me - 1 if side == 0 else me + 1},
            device_id_type=MESH,
        )

    def send_halo(k):
        for side in range(2):
            @pl.when(has[side])
            def _(side=side):
                halo_copy(k, side).start()

    send_halo(0)

    inverse = 1.0 / jnp.full((1, TILE), length[0], F32)

    def place_columns(sr, values):
        cm[0:GX] = jnp.concatenate([v[0] for v in values], axis=0)
        cm[GX : 2 * GX] = jnp.concatenate([v[1] for v in values], axis=0)
        turned = cm[...].T
        for c in range(GX):
            at = slice((c + 1) * TILE, (c + 2) * TILE)
            sc[0, sr, at, :] = jnp.broadcast_to(turned[:, c : c + 1], (TILE, TILE))
            sc[1, sr, at, :] = jnp.broadcast_to(turned[:, GX + c : GX + c + 1], (TILE, TILE))

    vx[...] = jnp.zeros_like(vx)
    cm[...] = jnp.zeros_like(cm)
    for sr in range(rows + 2):
        for edge in (0, (GX + 1) * TILE):
            sc[0, sr, edge : edge + TILE, :] = jnp.full((TILE, TILE), FAR, F32)
            sc[1, sr, edge : edge + TILE, :] = jnp.full((TILE, TILE), FAR, F32)
    for side, sr in ((0, 0), (1, rows + 1)):
        @pl.when(jnp.logical_not(has[side]))
        def _(sr=sr):
            sc[0, sr] = jnp.full((sc.shape[2], TILE), FAR, F32)
            sc[1, sr] = jnp.full((sc.shape[2], TILE), FAR, F32)

    def split(par, sr, at, value):
        high = value.astype(BF16)
        vx[par, sr, 0:PAD, at] = high
        vx[par, sr, PAD : 2 * PAD, at] = (value - high.astype(F32)).astype(BF16)

    own = pl.ds(TILE, row_lanes)
    for a in range(rows):
        base = a * row_lanes
        split(0, a + 1, own, pk[0, :, base : base + row_lanes])
        place_columns(
            a + 1,
            [
                (
                    (pk[0, RHS : RHS + 1, base + c * TILE : base + (c + 1) * TILE] + a) * inverse,
                    (pk[0, RHS + 1 : RHS + 2, base + c * TILE : base + (c + 1) * TILE] + c) * inverse,
                )
                for c in range(GX)
            ],
        )

    def build(a, c, srs):
        base = pl.multiple_of(a * row_lanes + c * TILE, TILE)
        here = pk[0, :, pl.ds(base, TILE)]
        tx = (here[RHS : RHS + 1] + a) * inverse
        ty = (here[RHS + 1 : RHS + 2] + c.astype(F32)) * inverse
        step = 64
        for sr in srs:
            for part in range(reach // step):
                at = pl.ds(pl.multiple_of(c * TILE + part * step, step), step)
                dx = sc[0, sr, at, :] - tx
                dy = sc[1, sr, at, :] - ty
                square = dx * dx + dy * dy
                close = jnp.maximum(1.0 - square * lax.rsqrt(jnp.maximum(square, TINY)), 0.0)
                twice = close * close
                w = twice * twice * (5.0 - 4.0 * close)
                high = w.astype(BF16)
                to = pl.ds((sr - a) * reach + part * step, step)
                whi[a, c, to, :] = high
                wlo[a, c, to, :] = (w - high.astype(F32)).astype(BF16)

    def dots(par, a, c, srs):
        lanes = pl.ds(pl.multiple_of(c * TILE, TILE), reach)
        v = jnp.concatenate([vx[par, sr, :, lanes] for sr in srs], axis=1)
        at = pl.ds((srs[0] - a) * reach, len(srs) * reach)
        r = jnp.dot(v, whi[a, c, at, :], preferred_element_type=F32)
        s = jnp.dot(v[:PAD], wlo[a, c, at, :], preferred_element_type=F32)
        return r[:PAD] + r[PAD:] + s

    def inner_rows(a):
        return [sr for sr in range(a, a + 3) if 1 <= sr <= rows]

    def outer_rows(a):
        return [sr for sr in range(a, a + 3) if sr < 1 or sr > rows]

    zero = jnp.zeros((PAD, TILE), F32)
    moments = []
    for k in range(3):
        par = k % 2

        def inner(c, carry, k=k, par=par):
            for a in range(rows):
                if k == 0:
                    build(a, c, inner_rows(a))
                at = pl.ds(pl.multiple_of(a * row_lanes + c * TILE, TILE), TILE)
                acc[:, at] = dots(par, a, c, inner_rows(a))
            return carry

        lax.fori_loop(0, GX, inner, 0)

        for side, sr in ((0, 0), (1, rows + 1)):
            @pl.when(has[side])
            def _(side=side, sr=sr, k=k, par=par):
                pltpu.make_async_remote_copy(
                    src_ref=pk.at[k, :, pl.ds(0, row_lanes)],
                    dst_ref=hv.at[k, side],
                    send_sem=halo_send.at[k, side],
                    recv_sem=halo_recv.at[k, side],
                    device_id={"rows": me - 1 if side == 0 else me + 1},
                    device_id_type=MESH,
                ).wait_recv()
                split(par, sr, own, hv[k, side])
                if k == 0:
                    place_columns(
                        sr,
                        [
                            (
                                (hv[0, side, RHS : RHS + 1, c * TILE : (c + 1) * TILE] + (sr - 1)) * inverse,
                                (hv[0, side, RHS + 1 : RHS + 2, c * TILE : (c + 1) * TILE] + c) * inverse,
                            )
                            for c in range(GX)
                        ],
                    )

        def outer(c, carry, k=k, par=par):
            first, cross, square = carry
            for a in range(rows):
                at = pl.ds(pl.multiple_of(a * row_lanes + c * TILE, TILE), TILE)
                total = acc[:, at]
                for sr in outer_rows(a):
                    if k == 0:
                        build(a, c, [sr])
                    total = total + dots(par, a, c, [sr])
                now = pk[k, :, at]
                later = amp * (total - now)
                if k == 0:
                    first = first + now * now
                cross = cross + now * later
                if k < 2:
                    square = square + later * later
                    pk[k + 1, :, at] = later
                    split(1 - par, a + 1, pl.ds(pl.multiple_of((c + 1) * TILE, TILE), TILE), later)
            return first, cross, square

        first, cross, square = lax.fori_loop(0, GX, outer, (zero, zero, zero))
        moments += ([first] if k == 0 else []) + [cross] + ([square] if k < 2 else [])
        if k < 2:
            send_halo(k + 1)

    lane = lax.broadcasted_iota(jnp.int32, (PAD, TILE), 1)
    packed = zero
    for i, part in enumerate(moments):
        packed = jnp.where(lane == i, jnp.sum(part, axis=1, keepdims=True), packed)
    mom[...] = packed
    gathered[me] = packed

    def mom_copy(k):
        peer = lax.rem(me + k, n)
        return pltpu.make_async_remote_copy(
            src_ref=mom,
            dst_ref=gathered.at[me],
            send_sem=mom_send.at[peer],
            recv_sem=mom_recv.at[me],
            device_id={"rows": peer},
            device_id_type=MESH,
        )

    def mom_start(k, carry):
        mom_copy(k).start()
        return carry

    lax.fori_loop(1, n, mom_start, 0)

    def mom_wait(k, carry):
        peer = lax.rem(me + k, n)
        pltpu.make_async_remote_copy(
            src_ref=mom,
            dst_ref=gathered.at[peer],
            send_sem=mom_send.at[peer],
            recv_sem=mom_recv.at[peer],
            device_id={"rows": peer},
            device_id_type=MESH,
        ).wait()
        return carry

    lax.fori_loop(1, n, mom_wait, 0)
    total = lax.fori_loop(0, n, lambda j, t: t + gathered[j], zero)

    m = [total[:, i : i + 1] for i in range(6)]
    a00, a01, a02 = (m[i + 1] + shift * m[i] for i in range(3))
    a11, a12 = (m[i + 1] + shift * m[i] for i in range(2, 4))
    a22 = m[5] + shift * m[4]
    l1 = a01 / a00
    l2 = a02 / a00
    b11 = a11 - l1 * a01
    b12 = a12 - l1 * a02
    b22 = a22 - l2 * a02
    g1 = m[1] - l1 * m[0]
    g2 = m[2] - l2 * m[0]
    fine1 = b11 > 1.0e-6 * a11
    safe1 = jnp.where(fine1, b11, 1.0)
    l3 = b12 / safe1
    d22 = b22 - l3 * b12
    fine2 = jnp.logical_and(fine1, d22 > 1.0e-6 * a22)
    c2 = jnp.where(fine2, (g2 - l3 * g1) / jnp.where(fine2, d22, 1.0), 0.0)
    c1 = jnp.where(fine1, (g1 - b12 * c2) / safe1, 0.0)
    c0 = (m[0] - a01 * c1 - a02 * c2) / a00
    q_ref[...] = jnp.broadcast_to((c0 * m[0] + c1 * m[1] + c2 * m[2]) / points, (PAD, TILE))

    for g in range(rows * GX):
        at = slice(g * TILE, (g + 1) * TILE)
        tiles[g] = c0 * pk[0, :, at] + c1 * pk[1, :, at] + c2 * pk[2, :, at]
    for s in range(rows * GX):
        found = tiles[cell[s]]
        x_ref[:, s * TILE : (s + 1) * TILE] = found[:RHS]

    for k in range(3):
        for side in range(2):
            @pl.when(has[side])
            def _(k=k, side=side):
                halo_copy(k, side).wait_send()


def shards(n, offsets, tile_cell, probes, target, lengthscale, amplitude, noise):
    tiles = tile_cell.shape[0]
    rows = tiles // GX
    places = jnp.arange(tiles, dtype=jnp.int32)
    order = jnp.sum(
        jnp.where(tile_cell[None, :] == places[:, None], places[None, :], 0), axis=1
    ).astype(jnp.int32)
    local = tiles * TILE
    width = (GX + 2) * TILE
    smem = pl.BlockSpec(memory_space=pltpu.SMEM)
    vmem = pl.BlockSpec(memory_space=pltpu.VMEM)
    solutions, quadratic = pl.pallas_call(
        functools.partial(kernel, n, rows, float(local * n)),
        out_shape=(
            jax.ShapeDtypeStruct((RHS, local), F32),
            jax.ShapeDtypeStruct((PAD, TILE), F32),
        ),
        in_specs=[smem] * 5 + [vmem] * 3,
        out_specs=(vmem, vmem),
        scratch_shapes=[
            pltpu.VMEM((tiles, PAD, TILE), F32),
            pltpu.VMEM((3, PAD, local), F32),
            pltpu.VMEM((3, 2, PAD, GX * TILE), F32),
            pltpu.VMEM((2, rows + 2, 2 * PAD, width), BF16),
            pltpu.VMEM((rows, GX, 9 * TILE, TILE), BF16),
            pltpu.VMEM((rows, GX, 9 * TILE, TILE), BF16),
            pltpu.VMEM((2, rows + 2, width, TILE), F32),
            pltpu.VMEM((TILE, TILE), F32),
            pltpu.VMEM((PAD, local), F32),
            pltpu.VMEM((PAD, TILE), F32),
            pltpu.VMEM((n, PAD, TILE), F32),
            pltpu.SemaphoreType.DMA((3, 2)),
            pltpu.SemaphoreType.DMA((3, 2)),
            pltpu.SemaphoreType.DMA((n,)),
            pltpu.SemaphoreType.DMA((n,)),
        ],
        compiler_params=pltpu.CompilerParams(
            collective_id=0, has_side_effects=True, vmem_limit_bytes=58 * 1024 * 1024
        ),
        name="solve",
    )(order, tile_cell, lengthscale, amplitude, noise, offsets, probes, target[None, :])
    return solutions, quadratic[:RHS, 0]


def solution(mesh):
    return jax.shard_map(
        functools.partial(shards, mesh.shape["rows"]),
        mesh=mesh,
        in_specs=(
            P(None, "rows"),
            P("rows"),
            P(None, "rows"),
            P("rows"),
            P("hyp"),
            P("hyp"),
            P("hyp"),
        ),
        out_specs=(P("hyp", "rows"), P("hyp")),
        check_vma=False,
    )
```

time: 302 us -> 61.3 us (0.20)
  matrix products: 144 us -> 0 us
  blocking collectives: 126 us -> 0 us
  Pallas kernels: 0 us -> 54.2 us
  starting transfers between devices: 15.7 us -> 0 us
  other arithmetic: 5.59 us -> 0.63 us
  waiting for transfers between devices: 4.11 us -> 0 us
    dot_general x27 -> x0, matrix products: 144 us -> none  [shifted_terms(): jnp.einsum('rabj,abij->rabi', values, weights, precision=lax.Precision.HI...]
    psum x4 -> x0, blocking collectives: 126 us -> none  [the longest x3 96.7 us: paired_sums(): lax.psum((local_sum(current, current), local_sum(current, image_now)), 'r...]
    pallas_call x0 -> x1, Pallas kernels: none -> 54.2 us  [shards(): pl.pallas_call(functools.partial(kernel, n, rows, float(local * n)), out_...]
    ppermute x8 -> x0, starting transfers between devices: 15.7 us -> none  [the longest x4 10.2 us: with_halo(): lax.ppermute(tail, axis, [(i, (i + 1) % count) for i in range(ends)])]
    ppermute x8 -> x0, waiting for transfers between devices: 4.11 us -> none  [the longest x4 4.1 us: with_halo(): lax.ppermute(head, axis, [((i + 1) % count, i) for i in range(ends)])]
  transfers between devices with their start and end apart: 8 -> 0, of which waited for: 3 -> 0; matrix products, arithmetic and copies ran while one was open for 1% -> 0% of each run, Pallas kernels for 0% -> 0%
where the time goes in v1:
time: 61.3 us; the launch traced here: 61 us
  Pallas kernels  54.2 us (88%)
  local copies, waits for them, and re-layouts  3.64 us (6%)
  between operations  2.59 us (4%)
  other arithmetic  0.63 us (1%)
    pallas_call x1, Pallas kernels, shards(): pl.pallas_call(functools.partial(kernel, n, rows, float(local * n)), out_...  54.2 us
    unnamed x3, local copies, waits for them, and re-layouts  2.32 us
    slice x1, local copies, waits for them, and re-layouts, shards(): return (solutions, quadratic[:RHS, 0])  1.32 us

profile of v1, /device:TPU:0, one launch (start us, length us, event | category | flops | bytes accessed | tf_op | source)
XLA Modules:
  0.0 61.0 jit_solution(5203404062727876406)
XLA Ops:
  2.6 0.0 copy-start
  2.6 0.6 %copy-done = s32[32]{0:T(128)S(1)} copy-done((s32[32]{0:T(128)S(1)}, s32[32]{0:T(128)}, u32[]{:S(2)}) %copy-start) | copy-done | bytes 152
  3.2 0.6 %select_reduce_fusion.order = s32[32]{0:T(128)} fusion(s32[32]{0:T(128)S(1)} %copy-done), kind=kLoop, calls=%fused_computation | loop fusion | flops 3040 | bytes 256 | tf_op jit(solution)/shard_map/reduce_sum | solution.py:299
  3.9 54.2 %solve.1 = (f32[9,4096]{1,0:T(8,128)}, f32[16,128]{1,0:T(8,128)}) custom-call(s32[32]{0:T(128)} %select_reduce_fusion.order, s32[32]{0:T(128)} %cell.1, f32[1]{0:T(128)S(6)} %copy.10.length, f32[1]{0:T(128)S(6)} %copy.11.amp_ref, f32[1]{0:T(128)S(6)} %copy.12.noise_ref, f32[2,4096]{1,0:T(2,128)} %off.1, s32[8,4096]{1,0:T(8,128)} %probes.1, f32[1,4096]{1,0:T(1,128)} %bitcast.1), custom_call_target="tpu_custom_call" | custom-call | tf_op jit(solution)/shard_map/solve/pallas_call | solution.py:306
  58.0 1.3 %slice_reduce_fusion = f32[9]{0:T(128)} fusion(f32[16,128]{1,0:T(8,128)} %get-tuple-element.5), kind=kLoop, calls=%fused_computation.2 | loop fusion | bytes 72 | tf_op jit(solution)/shard_map/slice | solution.py:336
  59.4 1.7 %copy.13 = f32[9,4096]{1,0:T(8,128)} copy(f32[9,4096]{1,0:T(8,128)} %get-tuple-element.8) | data formatting | bytes 294912
Async XLA Ops:
  2.6 0.7 %copy-start = (s32[32]{0:T(128)S(1)}, s32[32]{0:T(128)}, u32[]{:S(2)}) copy-start(s32[32]{0:T(128)} %cell.1) | copy-start | bytes 388

commit v2 on v1

--- a/solution.py
+++ b/solution.py
@@ -20,10 +20,10 @@
 
 def kernel(
     n, rows, points,
-    order, cell, length, amp_ref, noise_ref, off, probes, target,
+    order, cell, length, amp_ref, noise_ref, off_in, probes_in, target_in,
     x_ref, q_ref,
-    tiles, pk, hv, vx, whi, wlo, sc, cm, acc, mom, gathered,
-    halo_send, halo_recv, mom_send, mom_recv,
+    off, probes, target, tiles, pk, hv, vx, whi, wlo, ohi, olo, sc, cm, acc, mom, gathered,
+    load_sem, halo_send, halo_recv, mom_send, mom_recv,
 ):
     me = lax.axis_index("rows")
     has = (me > 0, me < n - 1)
@@ -41,6 +41,22 @@
         return carry
 
     lax.fori_loop(1, n, greet, 0)
+    loads = [
+        pltpu.make_async_copy(source, held, load_sem.at[i])
+        for i, (source, held) in enumerate(
+            ((off_in, off), (probes_in, probes), (target_in, target))
+        )
+    ]
+    for load in loads:
+        load.start()
+    vx[...] = jnp.zeros_like(vx)
+    cm[...] = jnp.zeros_like(cm)
+    for sr in range(rows + 2):
+        for edge in (0, (GX + 1) * TILE):
+            sc[0, sr, edge : edge + TILE, :] = jnp.full((TILE, TILE), FAR, F32)
+            sc[1, sr, edge : edge + TILE, :] = jnp.full((TILE, TILE), FAR, F32)
+    for load in loads:
+        load.wait()
 
     for g in range(rows * GX):
         lanes = slice(g * TILE, (g + 1) * TILE)
@@ -88,12 +104,6 @@
             sc[0, sr, at, :] = jnp.broadcast_to(turned[:, c : c + 1], (TILE, TILE))
             sc[1, sr, at, :] = jnp.broadcast_to(turned[:, GX + c : GX + c + 1], (TILE, TILE))
 
-    vx[...] = jnp.zeros_like(vx)
-    cm[...] = jnp.zeros_like(cm)
-    for sr in range(rows + 2):
-        for edge in (0, (GX + 1) * TILE):
-            sc[0, sr, edge : edge + TILE, :] = jnp.full((TILE, TILE), FAR, F32)
-            sc[1, sr, edge : edge + TILE, :] = jnp.full((TILE, TILE), FAR, F32)
     for side, sr in ((0, 0), (1, rows + 1)):
         @pl.when(jnp.logical_not(has[side]))
         def _(sr=sr):
@@ -120,51 +130,50 @@
             ],
         )
 
-    def build(a, c, srs):
+    def build(high_ref, low_ref, a, c, sr, first, lanes):
         base = pl.multiple_of(a * row_lanes + c * TILE, TILE)
         here = pk[0, :, pl.ds(base, TILE)]
         tx = (here[RHS : RHS + 1] + a) * inverse
         ty = (here[RHS + 1 : RHS + 2] + c.astype(F32)) * inverse
         step = 64
-        for sr in srs:
-            for part in range(reach // step):
-                at = pl.ds(pl.multiple_of(c * TILE + part * step, step), step)
-                dx = sc[0, sr, at, :] - tx
-                dy = sc[1, sr, at, :] - ty
-                square = dx * dx + dy * dy
-                close = jnp.maximum(1.0 - square * lax.rsqrt(jnp.maximum(square, TINY)), 0.0)
-                twice = close * close
-                w = twice * twice * (5.0 - 4.0 * close)
-                high = w.astype(BF16)
-                to = pl.ds((sr - a) * reach + part * step, step)
-                whi[a, c, to, :] = high
-                wlo[a, c, to, :] = (w - high.astype(F32)).astype(BF16)
-
-    def dots(par, a, c, srs):
-        lanes = pl.ds(pl.multiple_of(c * TILE, TILE), reach)
-        v = jnp.concatenate([vx[par, sr, :, lanes] for sr in srs], axis=1)
-        at = pl.ds((srs[0] - a) * reach, len(srs) * reach)
-        r = jnp.dot(v, whi[a, c, at, :], preferred_element_type=F32)
-        s = jnp.dot(v[:PAD], wlo[a, c, at, :], preferred_element_type=F32)
+        for part in range(reach // step):
+            at = pl.ds(pl.multiple_of(c * TILE + part * step, step), step)
+            dx = sc[0, sr, at, :] - tx
+            dy = sc[1, sr, at, :] - ty
+            square = dx * dx + dy * dy
+            close = jnp.maximum(1.0 - square * lax.rsqrt(jnp.maximum(square, TINY)), 0.0)
+            twice = close * close
+            w = twice * twice * (5.0 - 4.0 * close)
+            high = w.astype(BF16)
+            to = pl.ds(first + part * step, step)
+            high_ref[to, lanes] = high
+            low_ref[to, lanes] = (w - high.astype(F32)).astype(BF16)
+
+    def apply(v, high_ref, low_ref):
+        r = jnp.dot(v, high_ref[...], preferred_element_type=F32)
+        s = jnp.dot(v[:PAD], low_ref[...], preferred_element_type=F32)
         return r[:PAD] + r[PAD:] + s
 
-    def inner_rows(a):
-        return [sr for sr in range(a, a + 3) if 1 <= sr <= rows]
-
-    def outer_rows(a):
-        return [sr for sr in range(a, a + 3) if sr < 1 or sr > rows]
-
+    pair = 2 * TILE
     zero = jnp.zeros((PAD, TILE), F32)
     moments = []
     for k in range(3):
         par = k % 2
 
         def inner(c, carry, k=k, par=par):
+            if k == 0:
+                for sr in range(1, rows + 1):
+                    for a in range(rows):
+                        build(
+                            whi.at[c], wlo.at[c], a, c, sr, (sr - 1) * reach,
+                            slice(a * TILE, (a + 1) * TILE),
+                        )
+            lanes = pl.ds(pl.multiple_of(c * TILE, TILE), reach)
+            v = jnp.concatenate([vx[par, sr, :, lanes] for sr in range(1, rows + 1)], axis=1)
+            part = apply(v, whi.at[c], wlo.at[c])
             for a in range(rows):
-                if k == 0:
-                    build(a, c, inner_rows(a))
                 at = pl.ds(pl.multiple_of(a * row_lanes + c * TILE, TILE), TILE)
-                acc[:, at] = dots(par, a, c, inner_rows(a))
+                acc[:, at] = part[:, a * TILE : (a + 1) * TILE]
             return carry
 
         lax.fori_loop(0, GX, inner, 0)
@@ -195,13 +204,25 @@
 
         def outer(c, carry, k=k, par=par):
             first, cross, square = carry
+            sources = pl.ds(pl.multiple_of(c * pair, pair), 2 * pair)
             for a in range(rows):
-                at = pl.ds(pl.multiple_of(a * row_lanes + c * TILE, TILE), TILE)
+                at = pl.ds(pl.multiple_of(a * row_lanes + c * pair, pair), pair)
                 total = acc[:, at]
-                for sr in outer_rows(a):
+                for side, sr, edge in ((0, 0, 0), (1, rows + 1, rows - 1)):
+                    if a != edge:
+                        continue
                     if k == 0:
-                        build(a, c, [sr])
-                    total = total + dots(par, a, c, [sr])
+                        for held in (ohi, olo):
+                            held[side, c, 3 * TILE :, :TILE] = jnp.zeros((TILE, TILE), BF16)
+                            held[side, c, :TILE, TILE:] = jnp.zeros((TILE, TILE), BF16)
+                        for t in range(2):
+                            build(
+                                ohi.at[side, c], olo.at[side, c], a, 2 * c + t, sr, t * TILE,
+                                slice(t * TILE, (t + 1) * TILE),
+                            )
+                    total = total + apply(
+                        vx[par, sr, :, sources], ohi.at[side, c], olo.at[side, c]
+                    )
                 now = pk[k, :, at]
                 later = amp * (total - now)
                 if k == 0:
@@ -210,10 +231,11 @@
                 if k < 2:
                     square = square + later * later
                     pk[k + 1, :, at] = later
-                    split(1 - par, a + 1, pl.ds(pl.multiple_of((c + 1) * TILE, TILE), TILE), later)
+                    split(1 - par, a + 1, pl.ds(pl.multiple_of(c * pair + TILE, TILE), pair), later)
             return first, cross, square
 
-        first, cross, square = lax.fori_loop(0, GX, outer, (zero, zero, zero))
+        wide = jnp.zeros((PAD, pair), F32)
+        first, cross, square = lax.fori_loop(0, GX // 2, outer, (wide, wide, wide))
         moments += ([first] if k == 0 else []) + [cross] + ([square] if k < 2 else [])
         if k < 2:
             send_halo(k + 1)
@@ -276,7 +298,10 @@
     c2 = jnp.where(fine2, (g2 - l3 * g1) / jnp.where(fine2, d22, 1.0), 0.0)
     c1 = jnp.where(fine1, (g1 - b12 * c2) / safe1, 0.0)
     c0 = (m[0] - a01 * c1 - a02 * c2) / a00
-    q_ref[...] = jnp.broadcast_to((c0 * m[0] + c1 * m[1] + c2 * m[2]) / points, (PAD, TILE))
+    values = (c0 * m[0] + c1 * m[1] + c2 * m[2]) / points
+    sublane = lax.broadcasted_iota(jnp.int32, (PAD, TILE), 0)
+    turned = jnp.sum(jnp.where(lane == sublane, values, 0.0), axis=0, keepdims=True)
+    q_ref[...] = turned[:, :RHS]
 
     for g in range(rows * GX):
         at = slice(g * TILE, (g + 1) * TILE)
@@ -307,22 +332,28 @@
         functools.partial(kernel, n, rows, float(local * n)),
         out_shape=(
             jax.ShapeDtypeStruct((RHS, local), F32),
-            jax.ShapeDtypeStruct((PAD, TILE), F32),
+            jax.ShapeDtypeStruct((1, RHS), F32),
         ),
-        in_specs=[smem] * 5 + [vmem] * 3,
+        in_specs=[smem] * 5 + [pl.BlockSpec(memory_space=pl.ANY)] * 3,
         out_specs=(vmem, vmem),
         scratch_shapes=[
+            pltpu.VMEM((2, local), F32),
+            pltpu.VMEM((RHS - 1, local), jnp.int32),
+            pltpu.VMEM((1, local), F32),
             pltpu.VMEM((tiles, PAD, TILE), F32),
             pltpu.VMEM((3, PAD, local), F32),
             pltpu.VMEM((3, 2, PAD, GX * TILE), F32),
             pltpu.VMEM((2, rows + 2, 2 * PAD, width), BF16),
-            pltpu.VMEM((rows, GX, 9 * TILE, TILE), BF16),
-            pltpu.VMEM((rows, GX, 9 * TILE, TILE), BF16),
+            pltpu.VMEM((GX, rows * 3 * TILE, rows * TILE), BF16),
+            pltpu.VMEM((GX, rows * 3 * TILE, rows * TILE), BF16),
+            pltpu.VMEM((2, GX // 2, 4 * TILE, 2 * TILE), BF16),
+            pltpu.VMEM((2, GX // 2, 4 * TILE, 2 * TILE), BF16),
             pltpu.VMEM((2, rows + 2, width, TILE), F32),
             pltpu.VMEM((TILE, TILE), F32),
             pltpu.VMEM((PAD, local), F32),
             pltpu.VMEM((PAD, TILE), F32),
             pltpu.VMEM((n, PAD, TILE), F32),
+            pltpu.SemaphoreType.DMA((3,)),
             pltpu.SemaphoreType.DMA((3, 2)),
             pltpu.SemaphoreType.DMA((3, 2)),
             pltpu.SemaphoreType.DMA((n,)),
@@ -333,7 +364,7 @@
         ),
         name="solve",
     )(order, tile_cell, lengthscale, amplitude, noise, offsets, probes, target[None, :])
-    return solutions, quadratic[:RHS, 0]
+    return solutions, quadratic.reshape(RHS)
 
 
 def solution(mesh):

time: 61.3 us -> 56.3 us (0.918)
  Pallas kernels: 54.2 us -> 50 us
  local copies, waits for them, and re-layouts: 3.64 us -> 2.84 us
    pallas_call x1, Pallas kernels: 54.2 us -> 50 us  [shards(): pl.pallas_call(functools.partial(kernel, n, rows, float(local * n)), out_...]
    slice x1 -> x0, local copies, waits for them, and re-layouts: 1.32 us -> none  [shards(): return (solutions, quadratic[:RHS, 0])]
    unnamed x3 -> x6, local copies, waits for them, and re-layouts: 2.32 us -> 2.84 us
where the time goes in v2:
time: 56.3 us; the launch traced here: 56.1 us
  Pallas kernels  50 us (89%)
  local copies, waits for them, and re-layouts  2.84 us (5%)
  between operations  2.59 us (5%)
  other arithmetic  0.63 us (1%)
    pallas_call x1, Pallas kernels, shards(): pl.pallas_call(functools.partial(kernel, n, rows, float(local * n)), out_...  50 us
    unnamed x6, local copies, waits for them, and re-layouts  2.84 us

profile of v2, /device:TPU:0, one launch (start us, length us, event | category | flops | bytes accessed | tf_op | source)
XLA Modules:
  0.0 56.1 jit_solution(10915432183003220774)
XLA Ops:
  2.6 0.0 copy-start
  2.6 0.6 %copy-done = s32[32]{0:T(128)S(1)} copy-done((s32[32]{0:T(128)S(1)}, s32[32]{0:T(128)}, u32[]{:S(2)}) %copy-start) | copy-done | bytes 152
  3.2 0.6 %select_reduce_fusion.order = s32[32]{0:T(128)} fusion(s32[32]{0:T(128)S(1)} %copy-done), kind=kLoop, calls=%fused_computation | loop fusion | flops 3040 | bytes 256 | tf_op jit(solution)/shard_map/reduce_sum | solution.py:324
  3.9 50.0 %solve.1 = (f32[9,4096]{1,0:T(8,128)}, f32[1,9]{1,0:T(1,128)}) custom-call(s32[32]{0:T(128)} %select_reduce_fusion.order, s32[32]{0:T(128)} %cell.1, f32[1]{0:T(128)S(6)} %copy.11.length, f32[1]{0:T(128)S(6)} %copy.12.amp_ref, f32[1]{0:T(128)S(6)} %copy.13.noise_ref, f32[2,4096]{1,0:T(2,128)} %off_in.1, s32[8,4096]{1,0:T(8,128)} %probes_in.1, f32[1,4096]{1,0:T(1,128)} %bitcast.2), custom_call_target="tpu_custom_call" | custom-call | tf_op jit(solution)/shard_map/solve/pallas_call | solution.py:331
  53.9 0.0 copy-start.1
  53.9 1.7 %copy.14 = f32[9,4096]{1,0:T(8,128)} copy(f32[9,4096]{1,0:T(8,128)} %get-tuple-element.8) | data formatting | bytes 294912
  55.6 0.0 copy-done.1
  55.6 0.5 copy.15
Async XLA Ops:
  2.6 0.7 %copy-start = (s32[32]{0:T(128)S(1)}, s32[32]{0:T(128)}, u32[]{:S(2)}) copy-start(s32[32]{0:T(128)} %cell.1) | copy-start | bytes 388
  53.9 1.7 %copy-start.1 = (f32[1,9]{1,0:T(1,128)S(1)}, f32[1,9]{1,0:T(1,128)}, u32[]{:S(2)}) copy-start(f32[1,9]{1,0:T(1,128)} %get-tuple-element.5) | copy-start | bytes 112

commit v3 on v2

--- a/solution.py
+++ b/solution.py
@@ -130,7 +130,7 @@
             ],
         )
 
-    def build(high_ref, low_ref, a, c, sr, first, lanes):
+    def build(high_ref, low_ref, a, c, sr, first):
         base = pl.multiple_of(a * row_lanes + c * TILE, TILE)
         here = pk[0, :, pl.ds(base, TILE)]
         tx = (here[RHS : RHS + 1] + a) * inverse
@@ -146,12 +146,16 @@
             w = twice * twice * (5.0 - 4.0 * close)
             high = w.astype(BF16)
             to = pl.ds(first + part * step, step)
-            high_ref[to, lanes] = high
-            low_ref[to, lanes] = (w - high.astype(F32)).astype(BF16)
+            high_ref[to, :] = high
+            low_ref[to, :] = (w - high.astype(F32)).astype(BF16)
 
     def apply(v, high_ref, low_ref):
-        r = jnp.dot(v, high_ref[...], preferred_element_type=F32)
-        s = jnp.dot(v[:PAD], low_ref[...], preferred_element_type=F32)
+        high, low = (
+            jnp.concatenate([held[t] for t in range(held.shape[0])], axis=1)
+            for held in (high_ref, low_ref)
+        )
+        r = jnp.dot(v, high, preferred_element_type=F32)
+        s = jnp.dot(v[:PAD], low, preferred_element_type=F32)
         return r[:PAD] + r[PAD:] + s
 
     pair = 2 * TILE
@@ -164,10 +168,7 @@
             if k == 0:
                 for sr in range(1, rows + 1):
                     for a in range(rows):
-                        build(
-                            whi.at[c], wlo.at[c], a, c, sr, (sr - 1) * reach,
-                            slice(a * TILE, (a + 1) * TILE),
-                        )
+                        build(whi.at[c, a], wlo.at[c, a], a, c, sr, (sr - 1) * reach)
             lanes = pl.ds(pl.multiple_of(c * TILE, TILE), reach)
             v = jnp.concatenate([vx[par, sr, :, lanes] for sr in range(1, rows + 1)], axis=1)
             part = apply(v, whi.at[c], wlo.at[c])
@@ -176,7 +177,7 @@
                 acc[:, at] = part[:, a * TILE : (a + 1) * TILE]
             return carry
 
-        lax.fori_loop(0, GX, inner, 0)
+        lax.fori_loop(0, GX, inner, 0, unroll=2 if k == 0 else 8)
 
         for side, sr in ((0, 0), (1, rows + 1)):
             @pl.when(has[side])
@@ -213,12 +214,11 @@
                         continue
                     if k == 0:
                         for held in (ohi, olo):
-                            held[side, c, 3 * TILE :, :TILE] = jnp.zeros((TILE, TILE), BF16)
-                            held[side, c, :TILE, TILE:] = jnp.zeros((TILE, TILE), BF16)
+                            held[side, c, 0, 3 * TILE :] = jnp.zeros((TILE, TILE), BF16)
+                            held[side, c, 1, :TILE] = jnp.zeros((TILE, TILE), BF16)
                         for t in range(2):
                             build(
-                                ohi.at[side, c], olo.at[side, c], a, 2 * c + t, sr, t * TILE,
-                                slice(t * TILE, (t + 1) * TILE),
+                                ohi.at[side, c, t], olo.at[side, c, t], a, 2 * c + t, sr, t * TILE
                             )
                     total = total + apply(
                         vx[par, sr, :, sources], ohi.at[side, c], olo.at[side, c]
@@ -235,7 +235,7 @@
             return first, cross, square
 
         wide = jnp.zeros((PAD, pair), F32)
-        first, cross, square = lax.fori_loop(0, GX // 2, outer, (wide, wide, wide))
+        first, cross, square = lax.fori_loop(0, GX // 2, outer, (wide, wide, wide), unroll=1 if k == 0 else 8)
         moments += ([first] if k == 0 else []) + [cross] + ([square] if k < 2 else [])
         if k < 2:
             send_halo(k + 1)
@@ -344,10 +344,10 @@
             pltpu.VMEM((3, PAD, local), F32),
             pltpu.VMEM((3, 2, PAD, GX * TILE), F32),
             pltpu.VMEM((2, rows + 2, 2 * PAD, width), BF16),
-            pltpu.VMEM((GX, rows * 3 * TILE, rows * TILE), BF16),
-            pltpu.VMEM((GX, rows * 3 * TILE, rows * TILE), BF16),
-            pltpu.VMEM((2, GX // 2, 4 * TILE, 2 * TILE), BF16),
-            pltpu.VMEM((2, GX // 2, 4 * TILE, 2 * TILE), BF16),
+            pltpu.VMEM((GX, rows, rows * 3 * TILE, TILE), BF16),
+            pltpu.VMEM((GX, rows, rows * 3 * TILE, TILE), BF16),
+            pltpu.VMEM((2, GX // 2, 2, 4 * TILE, TILE), BF16),
+            pltpu.VMEM((2, GX // 2, 2, 4 * TILE, TILE), BF16),
             pltpu.VMEM((2, rows + 2, width, TILE), F32),
             pltpu.VMEM((TILE, TILE), F32),
             pltpu.VMEM((PAD, local), F32),

time: 56.3 us -> 52.3 us (0.929)
  Pallas kernels: 50 us -> 46 us
    pallas_call x1, Pallas kernels: 50 us -> 46 us  [shards(): pl.pallas_call(functools.partial(kernel, n, rows, float(local * n)), out_...]
where the time goes in v3:
time: 52.3 us; the launch traced here: 52.1 us
  Pallas kernels  46 us (88%)
  local copies, waits for them, and re-layouts  2.84 us (5%)
  between operations  2.59 us (5%)
  other arithmetic  0.63 us (1%)
    pallas_call x1, Pallas kernels, shards(): pl.pallas_call(functools.partial(kernel, n, rows, float(local * n)), out_...  46 us
    unnamed x6, local copies, waits for them, and re-layouts  2.84 us

profile of v3, /device:TPU:0, one launch (start us, length us, event | category | flops | bytes accessed | tf_op | source)
XLA Modules:
  0.0 52.1 jit_solution(3731514169165596611)
XLA Ops:
  2.6 0.0 copy-start
  2.6 0.6 %copy-done = s32[32]{0:T(128)S(1)} copy-done((s32[32]{0:T(128)S(1)}, s32[32]{0:T(128)}, u32[]{:S(2)}) %copy-start) | copy-done | bytes 152
  3.2 0.6 %select_reduce_fusion.order = s32[32]{0:T(128)} fusion(s32[32]{0:T(128)S(1)} %copy-done), kind=kLoop, calls=%fused_computation | loop fusion | flops 3040 | bytes 256 | tf_op jit(solution)/shard_map/reduce_sum | solution.py:324
  3.9 46.0 %solve.1 = (f32[9,4096]{1,0:T(8,128)}, f32[1,9]{1,0:T(1,128)}) custom-call(s32[32]{0:T(128)} %select_reduce_fusion.order, s32[32]{0:T(128)} %cell.1, f32[1]{0:T(128)S(6)} %copy.11.length, f32[1]{0:T(128)S(6)} %copy.12.amp_ref, f32[1]{0:T(128)S(6)} %copy.13.noise_ref, f32[2,4096]{1,0:T(2,128)} %off_in.1, s32[8,4096]{1,0:T(8,128)} %probes_in.1, f32[1,4096]{1,0:T(1,128)} %bitcast.2), custom_call_target="tpu_custom_call" | custom-call | tf_op jit(solution)/shard_map/solve/pallas_call | solution.py:331
  49.9 0.0 copy-start.1
  49.9 1.7 %copy.14 = f32[9,4096]{1,0:T(8,128)} copy(f32[9,4096]{1,0:T(8,128)} %get-tuple-element.8) | data formatting | bytes 294912
  51.6 0.0 copy-done.1
  51.6 0.5 copy.15
Async XLA Ops:
  2.6 0.7 %copy-start = (s32[32]{0:T(128)S(1)}, s32[32]{0:T(128)}, u32[]{:S(2)}) copy-start(s32[32]{0:T(128)} %cell.1) | copy-start | bytes 388
  49.9 1.7 %copy-start.1 = (f32[1,9]{1,0:T(1,128)S(1)}, f32[1,9]{1,0:T(1,128)}, u32[]{:S(2)}) copy-start(f32[1,9]{1,0:T(1,128)} %get-tuple-element.5) | copy-start | bytes 112
